TPU v7x, 32 devices: a whole 2x2x4 slice. The times are simulated.
32 devices in a mesh: tm: 4 (over y, x), slab: 8 (over z, core).
Axes of the slice: x: 2, y: 2, z: 4, core: 2. Of those that a mesh axis runs over, the one named last changes fastest.
Arguments:
- velocity: bfloat16 [4, 3, 2, 131072], P('tm', None, None, 'slab'), may hold values from -64 to 64
- shell_index: int32 [131072], P('slab'), may hold values from 0 to 127, as said below
- ref_order: int32 [4], replicated, may hold values from 0 to 3, each once
Outputs:
- coherence: float32 [4, 4, 128], P('tm')
- spectrum: float32 [4, 128], P('tm')
Inputs may be any that keep to these rules, and one draw needn't show every extreme that they name: `shell_index`: every shell number from 0 to 127 is taken by some mode. `ref_order`: each snapshot number appears once.
All inputs are finite; a program needn't handle non-finite values.
Results may differ from a plain program's by a relative error of at most 0.0003.
Values may be sent and summed in bfloat16 or wider, within the bound.
A program may use at most 64 MiB of HBM per device.

v0:
```python
import functools

import jax
import jax.numpy as jnp
from jax import lax
from jax.experimental import pallas as pl
from jax.experimental.pallas import tpu as pltpu
from jax.sharding import PartitionSpec as P

SHELLS = 128
LANES = 128
CORES = 2
MESH = pl.DeviceIdType.MESH


def kernel(
    snaps, slabs, rows,
    vel_ref, ids_ref, order_ref,
    coh_ref, spec_ref,
    staged, ids, order, got, split, terms, lhs, hot, mine, packs, near, mid, far, total, ready,
    load_sem, stage_sem, send_sem, recv_sem, near_send, near_recv, far_send, far_recv,
):
    tm = lax.axis_index("tm")
    slab = lax.axis_index("slab")
    core = lax.rem(slab, CORES)
    place = lax.div(slab, CORES)
    places = slabs // CORES
    pairs = snaps * snaps
    half = 3 * snaps // CORES

    others = []
    for high in reversed(range(snaps // 2)):
        for low in (1, 0):
            other_high = lax.rem(lax.div(tm, 2) + high, snaps // 2)
            others.append(other_high * 2 + lax.rem(lax.rem(tm, 2) + low, 2))
    others = others[:-1]
    other_core = CORES - 1 - core
    near_peers = [(other, other_core, 1) for other in others]
    near_peers += [(other, core, 0) for other in others]
    near_peers += [(tm, other_core, 1)]
    far_peers = []
    for offset in range(1, places):
        away = lax.rem(place + offset, places)
        far_peers += [(away, other_core, 1), (away, core, 0)]
    far_peers += [(place, other_core, 1)]

    barrier = pltpu.get_barrier_semaphore()
    for away, to_core, _ in far_peers[:-1]:
        pl.semaphore_signal(
            barrier, inc=1, device_id=(tm, away * CORES + to_core), device_id_type=MESH
        )
    for other, to_core, _ in near_peers:
        pl.semaphore_signal(
            barrier, inc=1, device_id=(other, place * CORES + to_core), device_id_type=MESH
        )

    def share_of(snap):
        return pl.ds(pl.multiple_of(snap * 2 * rows, 2 * rows), 2 * rows)

    for n, other in enumerate(others):
        pltpu.make_async_copy(vel_ref.at[:, share_of(other)], staged.at[n], stage_sem).start()
    load_own = pltpu.make_async_copy(vel_ref.at[:, share_of(tm)], got.at[tm], load_sem.at[0])
    load_own.start()
    load_ids = pltpu.make_async_copy(
        ids_ref.at[pl.ds(pl.multiple_of(tm * rows, rows), rows)], ids, load_sem.at[1]
    )
    load_ids.start()
    load_order = pltpu.make_async_copy(order_ref, order, load_sem.at[2])
    load_order.start()

    pl.semaphore_wait(barrier, len(near_peers) + len(far_peers) - 1)
    pltpu.make_async_copy(staged, staged, stage_sem).wait()
    for n, other in enumerate(others):
        move = pltpu.make_async_remote_copy(
            src_ref=staged.at[n],
            dst_ref=got.at[tm],
            send_sem=send_sem,
            recv_sem=recv_sem,
            device_id=(other, slab),
            device_id_type=MESH,
        )
        move.start()

    load_ids.wait()
    shell = lax.broadcasted_iota(jnp.int32, (SHELLS, LANES), 0)
    for j in range(rows):
        same = shell == jnp.broadcast_to(ids[j : j + 1, :], (SHELLS, LANES))
        hot[:, j * LANES : (j + 1) * LANES] = jnp.where(same, 1.0, 0.0).astype(jnp.bfloat16)

    load_order.wait()
    load_own.wait()
    pltpu.make_async_copy(staged, staged, recv_sem).wait()

    real, imag = {}, {}
    for t in range(snaps):
        for c in range(3):
            split[t * 3 + c] = got[t, c].astype(jnp.float32)
    for t in range(snaps):
        for c in range(3):
            real[t, c] = split[t * 3 + c, pl.ds(0, rows, stride=2), :]
            imag[t, c] = split[t * 3 + c, pl.ds(1, rows, stride=2), :]

    for t in range(snaps):
        for r in range(t, snaps):
            value = real[t, 0] * real[r, 0] + imag[t, 0] * imag[r, 0]
            for c in (1, 2):
                value = value + real[t, c] * real[r, c]
                value = value + imag[t, c] * imag[r, c]
            terms[(t * snaps + r) * rows : (t * snaps + r + 1) * rows] = value
            if r > t:
                value = imag[t, 0] * real[r, 0] - real[t, 0] * imag[r, 0]
                for c in (1, 2):
                    value = value + imag[t, c] * real[r, c]
                    value = value - real[t, c] * imag[r, c]
                terms[(r * snaps + t) * rows : (r * snaps + t + 1) * rows] = value
    for j in range(rows):
        block = terms[pl.ds(j, pairs, stride=rows), :]
        lhs[:, j * LANES : (j + 1) * LANES] = block.astype(jnp.bfloat16)
    mine[...] = lax.dot_general(
        lhs[...], hot[...], (((1,), (1,)), ((), ())), preferred_element_type=jnp.float32
    )

    mid_rows = snaps // 2
    for t in range(snaps):
        packs[t, 0, :snaps] = mine[t * snaps : (t + 1) * snaps, :]
        packs[t, 0, snaps:half] = mine[pl.ds(t, mid_rows, stride=snaps), :]
        packs[t, 1, :mid_rows] = mine[pl.ds(t + mid_rows * snaps, mid_rows, stride=snaps), :]
        packs[t, 1, mid_rows:half] = mine[pl.ds(0, snaps, stride=snaps + 1), :]

    for n, (other, to_core, _) in enumerate(near_peers):
        copy = pltpu.make_async_remote_copy(
            src_ref=packs.at[other, to_core],
            dst_ref=near.at[n * half : (n + 1) * half],
            send_sem=near_send,
            recv_sem=near_recv,
            device_id=(other, place * CORES + to_core),
            device_id_type=MESH,
        )
        copy.start()
    value = packs[tm, core]
    pltpu.make_async_copy(near, near, near_recv).wait()
    for n in range(len(near_peers)):
        value = value + near[n * half : (n + 1) * half]
    mid[...] = value

    for n, (away, to_core, _) in enumerate(far_peers):
        copy = pltpu.make_async_remote_copy(
            src_ref=mid,
            dst_ref=far.at[n * half : (n + 1) * half],
            send_sem=far_send,
            recv_sem=far_recv,
            device_id=(tm, away * CORES + to_core),
            device_id_type=MESH,
        )
        copy.start()
    sums = [mid[...], None]
    pltpu.make_async_copy(far, far, far_recv).wait()
    for n in range(len(far_peers)):
        turn = far_peers[n][2]
        term = far[n * half : (n + 1) * half]
        sums[turn] = term if sums[turn] is None else sums[turn] + term
    total[core] = sums[0]
    total[other_core] = sums[1]

    across = total[0, :snaps]
    own_spectrum = total[0, pl.ds(tm, 1), :]
    ready[:mid_rows] = total[0, snaps:half]
    ready[mid_rows:] = total[1, :mid_rows]
    down = ready[...]
    spectra = total[1, mid_rows:half]
    which = lax.broadcasted_iota(jnp.int32, (snaps, SHELLS), 0)
    down = jnp.where(which == tm, 0.0, down)
    ready[...] = (across * across + down * down) / (own_spectrum * spectra)
    for j in range(snaps):
        coh_ref[0, j : j + 1, :] = ready[pl.ds(order[j], 1), :]
    spec_ref[...] = own_spectrum
    pltpu.make_async_copy(staged, staged, send_sem).wait()
    pltpu.make_async_copy(near, near, near_send).wait()
    pltpu.make_async_copy(far, far, far_send).wait()


def put(coh_ref, spec_ref, coh_out, spec_out, sems):
    copies = [
        pltpu.make_async_copy(coh_ref, coh_out, sems.at[0]),
        pltpu.make_async_copy(spec_ref, spec_out, sems.at[1]),
    ]
    for copy in copies:
        copy.start()
    for copy in copies:
        copy.wait()


def body(velocity, shell_index, ref_order):
    snaps = lax.axis_size("tm")
    slabs = lax.axis_size("slab")
    modes = velocity.shape[3]
    blocks = modes // LANES
    rows = blocks // snaps
    pairs = snaps * snaps
    vel = velocity.reshape(3, 2, blocks, LANES).transpose(0, 2, 1, 3)
    vel = vel.reshape(3, 2 * blocks, LANES)
    ids = shell_index.reshape(blocks, LANES)
    near = snaps * CORES - 1
    far = slabs - 1
    half = 3 * snaps // CORES
    coherence, spectrum = pl.pallas_call(
        functools.partial(kernel, snaps, slabs, rows),
        out_shape=(
            pltpu.VMEM((1, snaps, SHELLS), jnp.float32),
            pltpu.VMEM((1, SHELLS), jnp.float32),
        ),
        in_specs=[
            pl.BlockSpec(memory_space=pl.ANY),
            pl.BlockSpec(memory_space=pl.ANY),
            pl.BlockSpec(memory_space=pl.ANY),
        ],
        out_specs=(
            pl.BlockSpec(memory_space=pltpu.VMEM),
            pl.BlockSpec(memory_space=pltpu.VMEM),
        ),
        scratch_shapes=[
            pltpu.VMEM((snaps - 1, 3, 2 * rows, LANES), jnp.bfloat16),
            pltpu.VMEM((rows, LANES), jnp.int32),
            pltpu.SMEM((snaps,), jnp.int32),
            pltpu.VMEM((snaps, 3, 2 * rows, LANES), jnp.bfloat16),
            pltpu.VMEM((snaps * 3, 2 * rows, LANES), jnp.float32),
            pltpu.VMEM((pairs * rows, LANES), jnp.float32),
            pltpu.VMEM((pairs, rows * LANES), jnp.bfloat16),
            pltpu.VMEM((SHELLS, rows * LANES), jnp.bfloat16),
            pltpu.VMEM((pairs, SHELLS), jnp.float32),
            pltpu.VMEM((snaps, CORES, half, SHELLS), jnp.float32),
            pltpu.VMEM((near * half, SHELLS), jnp.float32),
            pltpu.VMEM((half, SHELLS), jnp.float32),
            pltpu.VMEM((far * half, SHELLS), jnp.float32),
            pltpu.VMEM((CORES, half, SHELLS), jnp.float32),
            pltpu.VMEM((snaps, SHELLS), jnp.float32),
            pltpu.SemaphoreType.DMA((3,)),
            pltpu.SemaphoreType.DMA,
            pltpu.SemaphoreType.DMA,
            pltpu.SemaphoreType.DMA,
            pltpu.SemaphoreType.DMA,
            pltpu.SemaphoreType.DMA,
            pltpu.SemaphoreType.DMA,
            pltpu.SemaphoreType.DMA,
        ],
        compiler_params=pltpu.CompilerParams(collective_id=0, has_side_effects=True),
    )(vel, ids, ref_order)
    coherence = pltpu.with_memory_space_constraint(coherence, pltpu.VMEM)
    spectrum = pltpu.with_memory_space_constraint(spectrum, pltpu.VMEM)
    return pl.pallas_call(
        put,
        out_shape=(
            jax.ShapeDtypeStruct((1, snaps, SHELLS), jnp.float32),
            jax.ShapeDtypeStruct((1, SHELLS), jnp.float32),
        ),
        in_specs=[pl.BlockSpec(memory_space=pltpu.VMEM)] * 2,
        out_specs=(pl.BlockSpec(memory_space=pl.ANY),) * 2,
        scratch_shapes=[pltpu.SemaphoreType.DMA((2,))],
    )(coherence, spectrum)


def solution(mesh):
    in_specs = (P("tm", None, None, "slab"), P("slab"), P())
    out_specs = (P("tm", None, None), P("tm", None))
    return jax.shard_map(body, mesh=mesh, in_specs=in_specs, out_specs=out_specs, check_vma=False)
```

profile of v0, /device:TPU:0, one launch (start us, length us, event | category | flops | bytes accessed | tf_op | source)
XLA Modules:
  0.0 18.2 jit_solution(12161310935998976241)
XLA Ops:
  0.6 17.0 %shard_map.50 = (f32[1,4,128]{2,1,0:T(4,128)S(1)}, f32[1,128]{1,0:T(1,128)S(1)}) custom-call(bf16[3,256,128]{2,1,0:T(8,128)(2,1)} %bitcast.6, s32[128,128]{1,0:T(8,128)} %bitcast.7, s32[4]{0:T(128)} %order_ref.1), custom_call_target="tpu_custom_call" | custom-call | tf_op jit(solution)/shard_map/pallas_call | solution.py:206
  17.6 0.6 %shard_map.51 = (f32[1,4,128]{2,1,0:T(4,128)}, f32[1,128]{1,0:T(1,128)}) custom-call(f32[1,4,128]{2,1,0:T(4,128)S(1)} %get-tuple-element.4.coh_ref, f32[1,128]{1,0:T(1,128)S(1)} %get-tuple-element.5.spec_ref), custom_call_target="tpu_custom_call" | custom-call | tf_op jit(solution)/shard_map/pallas_call | solution.py:250
where the time goes:
time: 18.4 us; the launch traced here: 18.2 us
  Pallas kernels  17.6 us (96%)
  between operations  0.64 us (3%)
    pallas_call x1, Pallas kernels, body(): pl.pallas_call(functools.partial(kernel, snaps, slabs, rows), out_shape=(...  17 us
    pallas_call x1, Pallas kernels, body(): pl.pallas_call(put, out_shape=(jax.ShapeDtypeStruct((1, snaps, SHELLS), j...  0.6 us

commit v1 on v0

v1 whole, which is shorter than its diff:
```python
import functools

import jax
import jax.numpy as jnp
from jax import lax
from jax.experimental import pallas as pl
from jax.experimental.pallas import tpu as pltpu
from jax.sharding import PartitionSpec as P

SHELLS = 128
LANES = 128
CORES = 2
HUB = 1
CHUNKS = 2
MESH = pl.DeviceIdType.MESH


def kernel(
    snaps, slabs, rows, direct,
    vel_ref, ids_ref, order_ref,
    coh_ref, spec_ref,
    staged, ids, order, got, split, terms, lhs, hot, mine, packs, near, mid, far, rest, total, ready,
    load_sem, stage_sem, ids_send, ids_recv, send_sem, recv_sem, near_send, near_recv,
    far_send, far_recv, rest_send, rest_recv,
):
    tm = lax.axis_index("tm")
    slab = lax.axis_index("slab")
    core = lax.rem(slab, CORES)
    place = lax.div(slab, CORES)
    places = slabs // CORES
    pairs = snaps * snaps
    part = rows // CHUNKS
    hub = core == HUB
    leaf = core != HUB
    root = jnp.logical_and(tm == 0, place == 0)
    outer = place != 0

    others = []
    for high in reversed(range(snaps // 2)):
        for low in (1, 0):
            other_high = lax.rem(lax.div(tm, 2) + high, snaps // 2)
            others.append(other_high * 2 + lax.rem(lax.rem(tm, 2) + low, 2))
    others = others[:-1]
    aways = [lax.rem(place + offset, places) for offset in range(1, places)]

    def hub_of(snap, where):
        return (snap, where * CORES + HUB)

    def leaf_of(snap, where):
        return (snap, where * CORES + 1 - HUB)

    barrier = pltpu.get_barrier_semaphore()

    def tell(device):
        pl.semaphore_signal(barrier, inc=1, device_id=device, device_id_type=MESH)

    def share_of(snap):
        return pl.ds(pl.multiple_of(snap * 2 * rows, 2 * rows), 2 * rows)

    def send(src, dst, send_to, recv_at, device):
        pltpu.make_async_remote_copy(
            src_ref=src, dst_ref=dst, send_sem=send_to, recv_sem=recv_at,
            device_id=device, device_id_type=MESH,
        ).start()

    def drain(ref, sem):
        pltpu.make_async_copy(ref, ref, sem).wait()

    for away in aways:
        tell(hub_of(tm, away))

    @pl.when(hub)
    def _():
        for other in others:
            tell(hub_of(other, place))
            tell(leaf_of(other, place))
        tell(leaf_of(tm, place))

    @pl.when(leaf)
    def _():
        tell(hub_of(tm, place))

    if direct:
        @pl.when(root)
        def _():
            for snap in range(1, snaps):
                for where in range(1, places):
                    tell(hub_of(snap, where))

    load_ids = pltpu.make_async_copy(
        ids_ref.at[pl.ds(pl.multiple_of(tm * rows, rows), rows)], ids.at[HUB], load_sem.at[1]
    )
    load_order = pltpu.make_async_copy(order_ref, order, load_sem.at[2])
    for other in others:
        pltpu.make_async_copy(vel_ref.at[:, share_of(other)], staged.at[other], stage_sem).start()
    load_ids.start()

    def exchange(peers):
        for h in range(CHUNKS):
            for peer in peers:
                send(
                    staged.at[peer, :, pl.ds(h * 2 * part, 2 * part)], got.at[core, h, tm],
                    send_sem, recv_sem.at[core * CHUNKS + h], hub_of(peer, place),
                )

    @pl.when(leaf)
    def _():
        pltpu.make_async_copy(vel_ref.at[:, share_of(tm)], staged.at[tm], stage_sem).start()
        load_order.start()
        pl.semaphore_wait(barrier, snaps)
        drain(staged, stage_sem)
        exchange(others + [tm])
        load_ids.wait()
        send(ids.at[HUB], ids.at[1 - HUB], ids_send, ids_recv, hub_of(tm, place))

    @pl.when(hub)
    def _():
        for h in range(CHUNKS):
            pltpu.make_async_copy(
                vel_ref.at[:, pl.ds(pl.multiple_of((tm * CHUNKS + h) * 2 * part, 2 * part), 2 * part)],
                got.at[HUB, h, tm], load_sem.at[0],
            ).start()
        load_order.start()
        heard = (snaps - 1) + (places - 1) + places
        if direct:
            heard = heard + jnp.where(jnp.logical_and(tm != 0, outer), CORES, 0)
        pl.semaphore_wait(barrier, heard)
        drain(staged.at[pl.ds(0, snaps - 1)], stage_sem)
        exchange(others)

        load_ids.wait()
        shell = lax.broadcasted_iota(jnp.int32, (SHELLS, LANES), 0)

        def one_hot(unit):
            for j in range(rows):
                same = shell == jnp.broadcast_to(ids[unit, j : j + 1, :], (SHELLS, LANES))
                hot[unit, :, j * LANES : (j + 1) * LANES] = jnp.where(same, 1.0, 0.0).astype(jnp.bfloat16)

        one_hot(HUB)
        drain(ids.at[1 - HUB], ids_recv)
        one_hot(1 - HUB)
        drain(got.at[HUB, :, 0], load_sem.at[0])

        def work(unit, h, first):
            count = snaps - 1 if unit == HUB else snaps
            drain(got.at[unit, h, pl.ds(0, count)], recv_sem.at[unit * CHUNKS + h])
            real, imag = {}, {}
            for t in range(snaps):
                for c in range(3):
                    split[t * 3 + c] = got[unit, h, t, c].astype(jnp.float32)
            for t in range(snaps):
                for c in range(3):
                    real[t, c] = split[t * 3 + c, pl.ds(0, part, stride=2), :]
                    imag[t, c] = split[t * 3 + c, pl.ds(1, part, stride=2), :]
            for t in range(snaps):
                for r in range(t, snaps):
                    value = real[t, 0] * real[r, 0] + imag[t, 0] * imag[r, 0]
                    for c in (1, 2):
                        value = value + real[t, c] * real[r, c]
                        value = value + imag[t, c] * imag[r, c]
                    terms[(t * snaps + r) * part : (t * snaps + r + 1) * part] = value
                    if r > t:
                        value = imag[t, 0] * real[r, 0] - real[t, 0] * imag[r, 0]
                        for c in (1, 2):
                            value = value + imag[t, c] * real[r, c]
                            value = value - real[t, c] * imag[r, c]
                        terms[(r * snaps + t) * part : (r * snaps + t + 1) * part] = value
            for j in range(part):
                block = terms[pl.ds(j, pairs, stride=part), :]
                lhs[:, j * LANES : (j + 1) * LANES] = block.astype(jnp.bfloat16)
            value = lax.dot_general(
                lhs[...], hot[unit, :, h * part * LANES : (h + 1) * part * LANES],
                (((1,), (1,)), ((), ())), preferred_element_type=jnp.float32,
            )
            mine[...] = value if first else mine[...] + value

        first = True
        for h in range(CHUNKS):
            for unit in (HUB, 1 - HUB):
                work(unit, h, first)
                first = False

        diagonal = mine[pl.ds(0, snaps, stride=snaps + 1), :]
        for t in range(snaps):
            packs[t, :snaps] = mine[t * snaps : (t + 1) * snaps, :]
            packs[t, snaps : 2 * snaps] = mine[pl.ds(t, snaps, stride=snaps), :]
            packs[t, 2 * snaps :] = diagonal
        for other in others:
            send(packs.at[other], near.at[tm], near_send, near_recv, hub_of(other, place))
        if direct:
            @pl.when(outer)
            def _():
                slot = (place - 1) * snaps + tm
                send(packs.at[0], rest.at[slot], rest_send, rest_recv, leaf_of(0, 0))
                send(packs.at[0], rest.at[slot], rest_send, rest_recv, hub_of(0, 0))
        near[tm] = packs[tm]
        drain(near.at[pl.ds(0, snaps - 1)], near_recv)
        value = near[0]
        for t in range(1, snaps):
            value = value + near[t]
        mid[...] = value

        for away in aways:
            if direct:
                @pl.when(jnp.logical_or(tm != 0, away != 0))
                def _():
                    send(mid, far.at[place], far_send, far_recv, leaf_of(tm, away))
                    send(mid, far.at[place], far_send, far_recv, hub_of(tm, away))
            else:
                send(mid, far.at[place], far_send, far_recv, leaf_of(tm, away))
                send(mid, far.at[place], far_send, far_recv, hub_of(tm, away))
        send(mid, far.at[place], far_send, far_recv, leaf_of(tm, place))
        far[place] = mid[...]

    def gather():
        @pl.when(hub)
        def _():
            drain(far.at[pl.ds(0, places - 1)], far_recv)

        @pl.when(leaf)
        def _():
            drain(far.at[pl.ds(0, places)], far_recv)

        value = far[0]
        for where in range(1, places):
            value = value + far[where]
        total[...] = value

    if direct:
        @pl.when(root)
        def _():
            @pl.when(leaf)
            def _():
                drain(far.at[0], far_recv)

            drain(rest, rest_recv)
            value = far[0]
            for where in range(places - 1):
                share = rest[where * snaps]
                for t in range(1, snaps):
                    share = share + rest[where * snaps + t]
                value = value + share
            total[...] = value

        pl.when(jnp.logical_not(root))(gather)
    else:
        gather()

    load_order.wait()
    across = total[:snaps]
    down = total[snaps : 2 * snaps]
    spectra = total[2 * snaps :]
    own_spectrum = total[pl.ds(2 * snaps + tm, 1), :]
    which = lax.broadcasted_iota(jnp.int32, (snaps, SHELLS), 0)
    down = jnp.where(which == tm, 0.0, down)
    ready[...] = (across * across + down * down) / (own_spectrum * spectra)
    for j in range(snaps):
        coh_ref[0, j : j + 1, :] = ready[pl.ds(order[j], 1), :]
    spec_ref[...] = own_spectrum

    @pl.when(leaf)
    def _():
        drain(staged, send_sem)
        drain(ids.at[HUB], ids_send)

    @pl.when(hub)
    def _():
        drain(staged.at[pl.ds(0, snaps - 1)], send_sem)
        drain(near.at[pl.ds(0, snaps - 1)], near_send)
        if direct:
            short = jnp.logical_and(tm == 0, outer)

            @pl.when(short)
            def _():
                drain(far.at[pl.ds(0, 2 * places - 3)], far_send)

            @pl.when(jnp.logical_not(short))
            def _():
                drain(far.at[pl.ds(0, 2 * places - 1)], far_send)

            @pl.when(outer)
            def _():
                drain(rest.at[pl.ds(0, CORES)], rest_send)
        else:
            drain(far.at[pl.ds(0, 2 * places - 1)], far_send)


def put(coh_ref, spec_ref, coh_out, spec_out, sems):
    copies = [
        pltpu.make_async_copy(coh_ref, coh_out, sems.at[0]),
        pltpu.make_async_copy(spec_ref, spec_out, sems.at[1]),
    ]
    for copy in copies:
        copy.start()
    for copy in copies:
        copy.wait()


def body(velocity, shell_index, ref_order):
    snaps = lax.axis_size("tm")
    slabs = lax.axis_size("slab")
    places = slabs // CORES
    modes = velocity.shape[3]
    blocks = modes // LANES
    rows = blocks // snaps
    part = rows // CHUNKS
    pairs = snaps * snaps
    high = 3 * snaps
    direct = places * snaps <= 32 and places > 1
    vel = velocity.reshape(3, 2, blocks, LANES).transpose(0, 2, 1, 3)
    vel = vel.reshape(3, 2 * blocks, LANES)
    ids = shell_index.reshape(blocks, LANES)
    coherence, spectrum = pl.pallas_call(
        functools.partial(kernel, snaps, slabs, rows, direct),
        out_shape=(
            pltpu.VMEM((1, snaps, SHELLS), jnp.float32),
            pltpu.VMEM((1, SHELLS), jnp.float32),
        ),
        in_specs=[
            pl.BlockSpec(memory_space=pl.ANY),
            pl.BlockSpec(memory_space=pl.ANY),
            pl.BlockSpec(memory_space=pl.ANY),
        ],
        out_specs=(
            pl.BlockSpec(memory_space=pltpu.VMEM),
            pl.BlockSpec(memory_space=pltpu.VMEM),
        ),
        scratch_shapes=[
            pltpu.VMEM((snaps, 3, 2 * rows, LANES), jnp.bfloat16),
            pltpu.VMEM((CORES, rows, LANES), jnp.int32),
            pltpu.SMEM((snaps,), jnp.int32),
            pltpu.VMEM((CORES, CHUNKS, snaps, 3, 2 * part, LANES), jnp.bfloat16),
            pltpu.VMEM((snaps * 3, 2 * part, LANES), jnp.float32),
            pltpu.VMEM((pairs * part, LANES), jnp.float32),
            pltpu.VMEM((pairs, part * LANES), jnp.bfloat16),
            pltpu.VMEM((CORES, SHELLS, rows * LANES), jnp.bfloat16),
            pltpu.VMEM((pairs, SHELLS), jnp.float32),
            pltpu.VMEM((snaps, high, SHELLS), jnp.float32),
            pltpu.VMEM((snaps, high, SHELLS), jnp.float32),
            pltpu.VMEM((high, SHELLS), jnp.float32),
            pltpu.VMEM((2 * places, high, SHELLS), jnp.float32),
            pltpu.VMEM(((places - 1) * snaps if direct else 1, high, SHELLS), jnp.float32),
            pltpu.VMEM((high, SHELLS), jnp.float32),
            pltpu.VMEM((snaps, SHELLS), jnp.float32),
            pltpu.SemaphoreType.DMA((3,)),
            pltpu.SemaphoreType.DMA,
            pltpu.SemaphoreType.DMA,
            pltpu.SemaphoreType.DMA,
            pltpu.SemaphoreType.DMA,
            pltpu.SemaphoreType.DMA((CORES * CHUNKS,)),
            pltpu.SemaphoreType.DMA,
            pltpu.SemaphoreType.DMA,
            pltpu.SemaphoreType.DMA,
            pltpu.SemaphoreType.DMA,
            pltpu.SemaphoreType.DMA,
            pltpu.SemaphoreType.DMA,
        ],
        compiler_params=pltpu.CompilerParams(collective_id=0, has_side_effects=True),
    )(vel, ids, ref_order)
    coherence = pltpu.with_memory_space_constraint(coherence, pltpu.VMEM)
    spectrum = pltpu.with_memory_space_constraint(spectrum, pltpu.VMEM)
    return pl.pallas_call(
        put,
        out_shape=(
            jax.ShapeDtypeStruct((1, snaps, SHELLS), jnp.float32),
            jax.ShapeDtypeStruct((1, SHELLS), jnp.float32),
        ),
        in_specs=[pl.BlockSpec(memory_space=pltpu.VMEM)] * 2,
        out_specs=(pl.BlockSpec(memory_space=pl.ANY),) * 2,
        scratch_shapes=[pltpu.SemaphoreType.DMA((2,))],
    )(coherence, spectrum)


def solution(mesh):
    in_specs = (P("tm", None, None, "slab"), P("slab"), P())
    out_specs = (P("tm", None, None), P("tm", None))
    return jax.shard_map(body, mesh=mesh, in_specs=in_specs, out_specs=out_specs, check_vma=False)
```

time: 18.4 us -> 15 us (0.82)
  Pallas kernels: 17.6 us -> 14.2 us
    pallas_call x1, Pallas kernels: 17 us -> 13.6 us  [body(): pl.pallas_call(functools.partial(kernel, snaps, slabs, rows, direct), out...]
where the time goes in v1:
time: 15 us; the launch traced here: 14.8 us
  Pallas kernels  14.2 us (95%)
  between operations  0.64 us (4%)
    pallas_call x1, Pallas kernels, body(): pl.pallas_call(functools.partial(kernel, snaps, slabs, rows, direct), out...  13.6 us
    pallas_call x1, Pallas kernels, body(): pl.pallas_call(put, out_shape=(jax.ShapeDtypeStruct((1, snaps, SHELLS), j...  0.6 us

profile of v1, /device:TPU:0, one launch (start us, length us, event | category | flops | bytes accessed | tf_op | source)
XLA Modules:
  0.0 14.8 jit_solution(4661184917904752920)
XLA Ops:
  0.6 13.6 %shard_map.50 = (f32[1,4,128]{2,1,0:T(4,128)S(1)}, f32[1,128]{1,0:T(1,128)S(1)}) custom-call(bf16[3,256,128]{2,1,0:T(8,128)(2,1)} %bitcast.6, s32[128,128]{1,0:T(8,128)} %bitcast.7, s32[4]{0:T(128)} %order_ref.1), custom_call_target="tpu_custom_call" | custom-call | tf_op jit(solution)/shard_map/pallas_call | solution.py:313
  14.2 0.6 %shard_map.51 = (f32[1,4,128]{2,1,0:T(4,128)}, f32[1,128]{1,0:T(1,128)}) custom-call(f32[1,4,128]{2,1,0:T(4,128)S(1)} %get-tuple-element.4.coh_ref, f32[1,128]{1,0:T(1,128)S(1)} %get-tuple-element.5.spec_ref), custom_call_target="tpu_custom_call" | custom-call | tf_op jit(solution)/shard_map/pallas_call | solution.py:362

commit v2 on v1

v2 whole, which is shorter than its diff:
```python
import functools

import jax
import jax.numpy as jnp
from jax import lax
from jax.experimental import pallas as pl
from jax.experimental.pallas import tpu as pltpu
from jax.sharding import PartitionSpec as P

SHELLS = 128
LANES = 128
CORES = 2
HUB = 1
PART = 8
MESH = pl.DeviceIdType.MESH


def plan(rows):
    base = rows // PART
    skew = 1 if base >= 3 else 0
    low = base - skew
    slots = [(0, low - 1, 0)] if low > 1 else []
    slots += [(low - 1 + extra, 1, extra + 1) for extra in range(2 * skew)]
    slots.append((low - 1 + 2 * skew, 1, 0))
    return base, skew, low, slots


def kernel(
    snaps, slabs, rows,
    vel_ref, ids_ref, order_ref,
    coh_ref, spec_ref,
    staged, ids, order, got, split, terms, lhs, hot, mine, packs, inbox, total, ready,
    load_sem, stage_sem, ids_send, ids_recv, send_sem, recv_sem, pack_send, pack_recv,
    near_ok, far_ok,
):
    tm = lax.axis_index("tm")
    slab = lax.axis_index("slab")
    core = lax.rem(slab, CORES)
    place = lax.div(slab, CORES)
    places = slabs // CORES
    pairs = snaps * snaps
    blocks = rows * snaps
    base, skew, low, slots = plan(rows)
    hub = core == HUB
    leaf = core != HUB
    me = place * snaps + tm
    last = snaps - 1
    gate = tm == last

    others = []
    for high in reversed(range(snaps // 2)):
        for low_bit in (1, 0):
            other_high = lax.rem(lax.div(tm, 2) + high, snaps // 2)
            others.append(other_high * 2 + lax.rem(lax.rem(tm, 2) + low_bit, 2))
    others = others[:-1]
    aways = [lax.rem(place + offset, places) for offset in range(1, places)]

    def hub_of(snap, where):
        return (snap, where * CORES + HUB)

    def leaf_of(snap, where):
        return (snap, where * CORES + 1 - HUB)

    def count_of(snap):
        return base + jnp.where(snap == 0, skew, 0) - jnp.where(snap == last, skew, 0)

    def source_of(snap, slot):
        first = snap * base
        if skew:
            first = first + jnp.where(snap == 0, 0, skew)
        at = slots[slot][0]
        if slot == len(slots) - 1:
            at = count_of(snap) - 1
        return first + at

    def piece(start, units, scale):
        size = PART * scale
        return pl.ds(pl.multiple_of(start * size, size), units * size)

    barrier = pltpu.get_barrier_semaphore()

    def tell(device):
        pl.semaphore_signal(barrier, inc=1, device_id=device, device_id_type=MESH)

    def send(src, dst, send_to, recv_at, device):
        pltpu.make_async_remote_copy(
            src_ref=src, dst_ref=dst, send_sem=send_to, recv_sem=recv_at,
            device_id=device, device_id_type=MESH,
        ).start()

    def drain(ref, sem):
        pltpu.make_async_copy(ref, ref, sem).wait()

    def for_slots(snap, run):
        for slot, (_, _, need) in enumerate(slots):
            if need:
                pl.when(count_of(snap) >= low + need)(functools.partial(run, slot))
            else:
                run(slot)

    load_order = pltpu.make_async_copy(order_ref, order, load_sem.at[2])
    for part in range(snaps):
        span = pl.ds(part * 2 * rows, 2 * rows)
        pltpu.make_async_copy(vel_ref.at[:, span], staged.at[:, span], stage_sem).start()

    @pl.when(leaf)
    def _():
        @pl.when(gate)
        def _():
            tell(hub_of(tm, place))

        @pl.when(jnp.logical_not(gate))
        def _():
            tell(leaf_of(last, place))

    @pl.when(hub)
    def _():
        for other in others:
            tell(hub_of(other, place))
        for snap in range(last):
            tell(leaf_of(snap, place))

    for away in aways:
        tell(leaf_of(last, away))

    load_order.start()

    def load_ids(slot):
        at, units, _ = slots[slot]
        pltpu.make_async_copy(
            ids_ref.at[piece(source_of(tm, slot), units, 1)],
            ids.at[HUB, pl.ds(at * PART, units * PART)], load_sem.at[1],
        ).start()

    for_slots(tm, load_ids)

    def drain_ids(ref, sem):
        for units in range(low, low + 2 * skew + 1):
            @pl.when(count_of(tm) == units)
            def _():
                drain(ref.at[pl.ds(0, units * PART)], sem)

    def exchange(peers):
        for slot in range(len(slots)):
            for peer in peers:
                at, units, need = slots[slot]

                def ship(peer=peer, slot=slot, at=at, units=units):
                    send(
                        staged.at[:, piece(source_of(peer, slot), units, 2)],
                        got.at[core, tm, :, pl.ds(at * 2 * PART, units * 2 * PART)],
                        send_sem, recv_sem.at[core * len(slots) + slot], hub_of(peer, place),
                    )

                if need:
                    pl.when(count_of(peer) >= low + need)(ship)
                else:
                    ship()

    @pl.when(leaf)
    def _():
        drain_ids(ids.at[HUB], load_sem.at[1])

        @pl.when(gate)
        def _():
            pl.semaphore_wait(near_ok, 1)

        @pl.when(jnp.logical_not(gate))
        def _():
            pl.semaphore_wait(barrier, snaps)

        drain(staged, stage_sem)

        def ship_ids(slot):
            at, units, _ = slots[slot]
            span = pl.ds(at * PART, units * PART)
            send(ids.at[HUB, span], ids.at[1 - HUB, span], ids_send, ids_recv, hub_of(tm, place))

        for_slots(tm, ship_ids)
        exchange(others + [tm])

        @pl.when(gate)
        def _():
            pl.semaphore_wait(barrier, last + CORES * snaps * (places - 1))
            for snap in range(snaps):
                pl.semaphore_signal(
                    far_ok, inc=1, device_id=hub_of(snap, place), device_id_type=MESH
                )

    @pl.when(hub)
    def _():
        def load_own(slot):
            at, units, _ = slots[slot]
            pltpu.make_async_copy(
                vel_ref.at[:, piece(source_of(tm, slot), units, 2)],
                got.at[HUB, tm, :, pl.ds(at * 2 * PART, units * 2 * PART)], load_sem.at[0],
            ).start()

        for_slots(tm, load_own)
        pl.semaphore_wait(barrier, last + jnp.where(gate, 1, 0))

        @pl.when(gate)
        def _():
            pl.semaphore_signal(
                near_ok, inc=1, device_id=leaf_of(tm, place), device_id_type=MESH
            )

        drain(staged, stage_sem)
        exchange(others)
        mine[...] = jnp.zeros_like(mine)
        shell = lax.broadcasted_iota(jnp.int32, (SHELLS, LANES), 0)

        def one_hot(unit, slot):
            at, units, _ = slots[slot]
            for j in range(at * PART, (at + units) * PART):
                same = shell == jnp.broadcast_to(ids[unit, j : j + 1, :], (SHELLS, LANES))
                hot[unit, :, j * LANES : (j + 1) * LANES] = jnp.where(same, 1.0, 0.0).astype(jnp.bfloat16)

        drain_ids(ids.at[HUB], load_sem.at[1])
        for_slots(tm, functools.partial(one_hot, HUB))
        drain_ids(ids.at[1 - HUB], ids_recv)
        for_slots(tm, functools.partial(one_hot, 1 - HUB))
        for units in range(low, low + 2 * skew + 1):
            @pl.when(count_of(tm) == units)
            def _():
                drain(got.at[HUB, 0, :, pl.ds(0, units * 2 * PART)], load_sem.at[0])

        def prepare(unit, at, row):
            span = pl.ds(at * 2 * PART, 2 * PART)
            real, imag = {}, {}
            for t in range(snaps):
                for c in range(3):
                    split[row, t * 3 + c] = got[unit, t, c, span, :].astype(jnp.float32)
            for t in range(snaps):
                for c in range(3):
                    real[t, c] = split[row, t * 3 + c, pl.ds(0, PART, stride=2), :]
                    imag[t, c] = split[row, t * 3 + c, pl.ds(1, PART, stride=2), :]
            for t in range(snaps):
                for r in range(t, snaps):
                    value = real[t, 0] * real[r, 0] + imag[t, 0] * imag[r, 0]
                    for c in (1, 2):
                        value = value + real[t, c] * real[r, c]
                        value = value + imag[t, c] * imag[r, c]
                    terms[row, (t * snaps + r) * PART : (t * snaps + r + 1) * PART] = value
                    if r > t:
                        value = imag[t, 0] * real[r, 0] - real[t, 0] * imag[r, 0]
                        for c in (1, 2):
                            value = value + imag[t, c] * real[r, c]
                            value = value - real[t, c] * imag[r, c]
                        terms[row, (r * snaps + t) * PART : (r * snaps + t + 1) * PART] = value
            for j in range(PART):
                block = terms[row, pl.ds(j, pairs, stride=PART), :]
                lhs[row, :, j * LANES : (j + 1) * LANES] = block.astype(jnp.bfloat16)

        wide = PART * LANES // 2

        def work(slot):
            at, units, _ = slots[slot]
            span = pl.ds(at * 2 * PART, units * 2 * PART)
            jobs = []
            for unit in (HUB, 1 - HUB):
                senders = snaps - 1 if unit == HUB else snaps
                drain(got.at[unit, pl.ds(0, senders), :, span], recv_sem.at[unit * len(slots) + slot])
                for step in range(units):
                    row = len(jobs)
                    prepare(unit, at + step, row)
                    jobs.append((unit, at + step, row))
            for side in range(2):
                value = mine[side]
                for unit, spot, row in jobs:
                    start = spot * PART * LANES + side * wide
                    value = value + lax.dot_general(
                        lhs[row, :, side * wide : (side + 1) * wide], hot[unit, :, start : start + wide],
                        (((1,), (1,)), ((), ())), preferred_element_type=jnp.float32,
                    )
                mine[side] = value

        for_slots(tm, work)

        def row_of(index):
            return mine[0, index, :] + mine[1, index, :]

        diagonal = row_of(pl.ds(0, snaps, stride=snaps + 1))
        for t in range(snaps):
            packs[t, :snaps] = row_of(pl.ds(t * snaps, snaps))
            packs[t, snaps : 2 * snaps] = row_of(pl.ds(t, snaps, stride=snaps))
            packs[t, 2 * snaps :] = diagonal
        pl.semaphore_wait(far_ok, 1)
        for where in range(places):
            for snap in range(snaps):
                send(packs.at[snap], inbox.at[me], pack_send, pack_recv, leaf_of(snap, where))

                @pl.when(me != where * snaps + snap)
                def _():
                    send(packs.at[snap], inbox.at[me], pack_send, pack_recv, hub_of(snap, where))
        inbox[me] = packs[tm]
        drain(inbox.at[pl.ds(0, snaps * places - 1)], pack_recv)

    @pl.when(leaf)
    def _():
        drain(inbox.at[pl.ds(0, snaps * places)], pack_recv)

    value = inbox[0]
    for n in range(1, snaps * places):
        value = value + inbox[n]
    total[...] = value

    load_order.wait()
    across = total[:snaps]
    down = total[snaps : 2 * snaps]
    spectra = total[2 * snaps :]
    own_spectrum = total[pl.ds(2 * snaps + tm, 1), :]
    which = lax.broadcasted_iota(jnp.int32, (snaps, SHELLS), 0)
    down = jnp.where(which == tm, 0.0, down)
    ready[...] = (across * across + down * down) / (own_spectrum * spectra)
    for j in range(snaps):
        coh_ref[0, j : j + 1, :] = ready[pl.ds(order[j], 1), :]
    spec_ref[...] = own_spectrum

    @pl.when(leaf)
    def _():
        drain(staged, send_sem)
        drain_ids(ids.at[HUB], ids_send)

    @pl.when(hub)
    def _():
        for units in range(low, low + 2 * skew + 1):
            @pl.when(count_of(tm) == units)
            def _():
                drain(staged.at[:, pl.ds(0, 2 * (blocks - units * PART))], send_sem)
        drain(inbox.at[pl.ds(0, 2 * snaps * places - 1)], pack_send)


def put(coh_ref, spec_ref, coh_out, spec_out, sems):
    copies = [
        pltpu.make_async_copy(coh_ref, coh_out, sems.at[0]),
        pltpu.make_async_copy(spec_ref, spec_out, sems.at[1]),
    ]
    for copy in copies:
        copy.start()
    for copy in copies:
        copy.wait()


def body(velocity, shell_index, ref_order):
    snaps = lax.axis_size("tm")
    slabs = lax.axis_size("slab")
    places = slabs // CORES
    modes = velocity.shape[3]
    blocks = modes // LANES
    rows = blocks // snaps
    _, skew, low, slots = plan(rows)
    most = slots[-1][0] + 1
    jobs = CORES * max(units for _, units, _ in slots)
    pairs = snaps * snaps
    high = 3 * snaps
    vel = velocity.reshape(3, 2, blocks, LANES).transpose(0, 2, 1, 3)
    vel = vel.reshape(3, 2 * blocks, LANES)
    ids = shell_index.reshape(blocks, LANES)
    coherence, spectrum = pl.pallas_call(
        functools.partial(kernel, snaps, slabs, rows),
        out_shape=(
            pltpu.VMEM((1, snaps, SHELLS), jnp.float32),
            pltpu.VMEM((1, SHELLS), jnp.float32),
        ),
        in_specs=[
            pl.BlockSpec(memory_space=pl.ANY),
            pl.BlockSpec(memory_space=pl.ANY),
            pl.BlockSpec(memory_space=pl.ANY),
        ],
        out_specs=(
            pl.BlockSpec(memory_space=pltpu.VMEM),
            pl.BlockSpec(memory_space=pltpu.VMEM),
        ),
        scratch_shapes=[
            pltpu.VMEM((3, 2 * blocks, LANES), jnp.bfloat16),
            pltpu.VMEM((CORES, most * PART, LANES), jnp.int32),
            pltpu.SMEM((snaps,), jnp.int32),
            pltpu.VMEM((CORES, snaps, 3, most * 2 * PART, LANES), jnp.bfloat16),
            pltpu.VMEM((jobs, snaps * 3, 2 * PART, LANES), jnp.float32),
            pltpu.VMEM((jobs, pairs * PART, LANES), jnp.float32),
            pltpu.VMEM((jobs, pairs, PART * LANES), jnp.bfloat16),
            pltpu.VMEM((CORES, SHELLS, most * PART * LANES), jnp.bfloat16),
            pltpu.VMEM((2, pairs, SHELLS), jnp.float32),
            pltpu.VMEM((snaps, high, SHELLS), jnp.float32),
            pltpu.VMEM((2 * snaps * places, high, SHELLS), jnp.float32),
            pltpu.VMEM((high, SHELLS), jnp.float32),
            pltpu.VMEM((snaps, SHELLS), jnp.float32),
            pltpu.SemaphoreType.DMA((3,)),
            pltpu.SemaphoreType.DMA,
            pltpu.SemaphoreType.DMA,
            pltpu.SemaphoreType.DMA,
            pltpu.SemaphoreType.DMA,
            pltpu.SemaphoreType.DMA((CORES * len(slots),)),
            pltpu.SemaphoreType.DMA,
            pltpu.SemaphoreType.DMA,
            pltpu.SemaphoreType.REGULAR,
            pltpu.SemaphoreType.REGULAR,
        ],
        compiler_params=pltpu.CompilerParams(collective_id=0, has_side_effects=True),
    )(vel, ids, ref_order)
    coherence = pltpu.with_memory_space_constraint(coherence, pltpu.VMEM)
    spectrum = pltpu.with_memory_space_constraint(spectrum, pltpu.VMEM)
    return pl.pallas_call(
        put,
        out_shape=(
            jax.ShapeDtypeStruct((1, snaps, SHELLS), jnp.float32),
            jax.ShapeDtypeStruct((1, SHELLS), jnp.float32),
        ),
        in_specs=[pl.BlockSpec(memory_space=pltpu.VMEM)] * 2,
        out_specs=(pl.BlockSpec(memory_space=pl.ANY),) * 2,
        scratch_shapes=[pltpu.SemaphoreType.DMA((2,))],
    )(coherence, spectrum)


def solution(mesh):
    in_specs = (P("tm", None, None, "slab"), P("slab"), P())
    out_specs = (P("tm", None, None), P("tm", None))
    return jax.shard_map(body, mesh=mesh, in_specs=in_specs, out_specs=out_specs, check_vma=False)
```

time: 15 us -> 14.7 us (0.980)
  Pallas kernels: 14.2 us -> 13.9 us
    pallas_call x1, Pallas kernels: 13.6 us -> 13.3 us  [body(): pl.pallas_call(functools.partial(kernel, snaps, slabs, rows), out_shape=(...]
where the time goes in v2:
time: 14.7 us; the launch traced here: 14.6 us
  Pallas kernels  13.9 us (95%)
  between operations  0.64 us (4%)
    pallas_call x1, Pallas kernels, body(): pl.pallas_call(functools.partial(kernel, snaps, slabs, rows), out_shape=(...  13.3 us
    pallas_call x1, Pallas kernels, body(): pl.pallas_call(put, out_shape=(jax.ShapeDtypeStruct((1, snaps, SHELLS), j...  0.6 us

profile of v2, /device:TPU:0, one launch (start us, length us, event | category | flops | bytes accessed | tf_op | source)
XLA Modules:
  0.0 14.6 jit_solution(9096511769499242033)
XLA Ops:
  0.6 13.3 %shard_map.50 = (f32[1,4,128]{2,1,0:T(4,128)S(1)}, f32[1,128]{1,0:T(1,128)S(1)}) custom-call(bf16[3,256,128]{2,1,0:T(8,128)(2,1)} %bitcast.6, s32[128,128]{1,0:T(8,128)} %bitcast.7, s32[4]{0:T(128)} %order_ref.1), custom_call_target="tpu_custom_call" | custom-call | tf_op jit(solution)/shard_map/pallas_call | solution.py:360
  14.0 0.6 %shard_map.51 = (f32[1,4,128]{2,1,0:T(4,128)}, f32[1,128]{1,0:T(1,128)}) custom-call(f32[1,4,128]{2,1,0:T(4,128)S(1)} %get-tuple-element.4.coh_ref, f32[1,128]{1,0:T(1,128)S(1)} %get-tuple-element.5.spec_ref), custom_call_target="tpu_custom_call" | custom-call | tf_op jit(solution)/shard_map/pallas_call | solution.py:404

commit v3 on v2

--- a/solution.py
+++ b/solution.py
@@ -31,7 +31,7 @@
     coh_ref, spec_ref,
     staged, ids, order, got, split, terms, lhs, hot, mine, packs, inbox, total, ready,
     load_sem, stage_sem, ids_send, ids_recv, send_sem, recv_sem, pack_send, pack_recv,
-    near_ok, far_ok,
+    near_ok, far_ok, late_ok,
 ):
     tm = lax.axis_index("tm")
     slab = lax.axis_index("slab")
@@ -46,6 +46,7 @@
     me = place * snaps + tm
     last = snaps - 1
     gate = tm == last
+    head = tm == 0
 
     others = []
     for high in reversed(range(snaps // 2)):
@@ -62,12 +63,14 @@
         return (snap, where * CORES + 1 - HUB)
 
     def count_of(snap):
+        if isinstance(snap, int):
+            return base + (skew if snap == 0 else 0) - (skew if snap == last else 0)
         return base + jnp.where(snap == 0, skew, 0) - jnp.where(snap == last, skew, 0)
 
     def source_of(snap, slot):
         first = snap * base
         if skew:
-            first = first + jnp.where(snap == 0, 0, skew)
+            first = first + (jnp.where(snap == 0, 0, skew) if not isinstance(snap, int) else (skew if snap else 0))
         at = slots[slot][0]
         if slot == len(slots) - 1:
             at = count_of(snap) - 1
@@ -75,6 +78,8 @@
 
     def piece(start, units, scale):
         size = PART * scale
+        if isinstance(start, int):
+            return pl.ds(start * size, units * size)
         return pl.ds(pl.multiple_of(start * size, size), units * size)
 
     barrier = pltpu.get_barrier_semaphore()
@@ -113,11 +118,26 @@
         def _():
             tell(leaf_of(last, place))
 
+        @pl.when(head)
+        def _():
+            tell(hub_of(tm, place))
+
     @pl.when(hub)
     def _():
-        for other in others:
-            tell(hub_of(other, place))
-        for snap in range(last):
+        @pl.when(gate)
+        def _():
+            tell(leaf_of(0, place))
+            for snap in range(1, last):
+                tell(hub_of(snap, place))
+
+        @pl.when(jnp.logical_not(gate))
+        def _():
+            for snap in range(snaps):
+                @pl.when(tm != snap)
+                def _():
+                    tell(hub_of(snap, place))
+
+        for snap in range(1, last):
             tell(leaf_of(snap, place))
 
     for away in aways:
@@ -152,7 +172,10 @@
                         send_sem, recv_sem.at[core * len(slots) + slot], hub_of(peer, place),
                     )
 
-                if need:
+                if need and isinstance(peer, int):
+                    if count_of(peer) >= low + need:
+                        ship()
+                elif need:
                     pl.when(count_of(peer) >= low + need)(ship)
                 else:
                     ship()
@@ -161,11 +184,11 @@
     def _():
         drain_ids(ids.at[HUB], load_sem.at[1])
 
-        @pl.when(gate)
+        @pl.when(jnp.logical_or(gate, head))
         def _():
             pl.semaphore_wait(near_ok, 1)
 
-        @pl.when(jnp.logical_not(gate))
+        @pl.when(jnp.logical_not(jnp.logical_or(gate, head)))
         def _():
             pl.semaphore_wait(barrier, snaps)
 
@@ -177,7 +200,19 @@
             send(ids.at[HUB, span], ids.at[1 - HUB, span], ids_send, ids_recv, hub_of(tm, place))
 
         for_slots(tm, ship_ids)
-        exchange(others + [tm])
+
+        @pl.when(head)
+        def _():
+            exchange(list(range(1, last)) + [0])
+            pl.semaphore_wait(barrier, 1)
+            pl.semaphore_signal(
+                late_ok, inc=1, device_id=hub_of(tm, place), device_id_type=MESH
+            )
+            exchange([last])
+
+        @pl.when(jnp.logical_not(head))
+        def _():
+            exchange(others + [tm])
 
         @pl.when(gate)
         def _():
@@ -199,25 +234,46 @@
         for_slots(tm, load_own)
         pl.semaphore_wait(barrier, last + jnp.where(gate, 1, 0))
 
-        @pl.when(gate)
+        @pl.when(jnp.logical_or(gate, head))
         def _():
             pl.semaphore_signal(
                 near_ok, inc=1, device_id=leaf_of(tm, place), device_id_type=MESH
             )
 
         drain(staged, stage_sem)
-        exchange(others)
-        mine[...] = jnp.zeros_like(mine)
+
+        @pl.when(head)
+        def _():
+            exchange(list(range(1, last)))
+
+        @pl.when(jnp.logical_not(head))
+        def _():
+            exchange(others)
+
         shell = lax.broadcasted_iota(jnp.int32, (SHELLS, LANES), 0)
+
+        def spot(j):
+            high, wide = divmod(j % PART, PART // 2)
+            half, lane = divmod(wide, 2)
+            return high, half, pl.ds(lane * LANES, LANES)
 
         def one_hot(unit, slot):
             at, units, _ = slots[slot]
             for j in range(at * PART, (at + units) * PART):
                 same = shell == jnp.broadcast_to(ids[unit, j : j + 1, :], (SHELLS, LANES))
-                hot[unit, :, j * LANES : (j + 1) * LANES] = jnp.where(same, 1.0, 0.0).astype(jnp.bfloat16)
+                mxu, half, lanes = spot(j)
+                hot[unit, j // PART, mxu, half * SHELLS : (half + 1) * SHELLS, lanes] = jnp.where(
+                    same, 1.0, 0.0
+                ).astype(jnp.bfloat16)
 
         drain_ids(ids.at[HUB], load_sem.at[1])
         for_slots(tm, functools.partial(one_hot, HUB))
+
+        @pl.when(head)
+        def _():
+            pl.semaphore_wait(late_ok, 1)
+            exchange([last])
+
         drain_ids(ids.at[1 - HUB], ids_recv)
         for_slots(tm, functools.partial(one_hot, 1 - HUB))
         for units in range(low, low + 2 * skew + 1):
@@ -250,40 +306,55 @@
                         terms[row, (r * snaps + t) * PART : (r * snaps + t + 1) * PART] = value
             for j in range(PART):
                 block = terms[row, pl.ds(j, pairs, stride=PART), :]
-                lhs[row, :, j * LANES : (j + 1) * LANES] = block.astype(jnp.bfloat16)
-
-        wide = PART * LANES // 2
-
-        def work(slot):
-            at, units, _ = slots[slot]
-            span = pl.ds(at * 2 * PART, units * 2 * PART)
+                mxu, half, lanes = spot(j)
+                lhs[row, mxu, half * pairs : (half + 1) * pairs, lanes] = block.astype(jnp.bfloat16)
+
+        def reduce(count, *sums):
             jobs = []
-            for unit in (HUB, 1 - HUB):
-                senders = snaps - 1 if unit == HUB else snaps
-                drain(got.at[unit, pl.ds(0, senders), :, span], recv_sem.at[unit * len(slots) + slot])
-                for step in range(units):
-                    row = len(jobs)
-                    prepare(unit, at + step, row)
-                    jobs.append((unit, at + step, row))
-            for side in range(2):
-                value = mine[side]
-                for unit, spot, row in jobs:
-                    start = spot * PART * LANES + side * wide
-                    value = value + lax.dot_general(
-                        lhs[row, :, side * wide : (side + 1) * wide], hot[unit, :, start : start + wide],
-                        (((1,), (1,)), ((), ())), preferred_element_type=jnp.float32,
+            for slot, (at, units, need) in enumerate(slots):
+                if low + need <= count:
+                    for unit in (HUB, 1 - HUB):
+                        for step in range(units):
+                            jobs.append((unit, slot, at + step, step == 0))
+
+            def stage(n):
+                unit, _, at, _ = jobs[n]
+                for mxu in range(2):
+                    pltpu.matmul_push_rhs(hot[unit, at, mxu], n % 2, mxu, transpose=True)
+
+            stage(0)
+            for n, (unit, slot, at, fresh) in enumerate(jobs):
+                if fresh:
+                    first, units, _ = slots[slot]
+                    senders = snaps - 1 if unit == HUB else snaps
+                    span = pl.ds(first * 2 * PART, units * 2 * PART)
+                    drain(
+                        got.at[unit, pl.ds(0, senders), :, span], recv_sem.at[unit * len(slots) + slot]
                     )
-                mine[side] = value
-
-        for_slots(tm, work)
-
-        def row_of(index):
-            return mine[0, index, :] + mine[1, index, :]
-
-        diagonal = row_of(pl.ds(0, snaps, stride=snaps + 1))
+                if n + 1 < len(jobs):
+                    stage(n + 1)
+                prepare(unit, at, n % 2)
+                for mxu in range(2):
+                    pltpu.matmul_acc_lhs(sums[mxu], lhs[n % 2, mxu], load_staged_rhs=n % 2)
+
+        def multiply(*sums):
+            for mxu in range(2):
+                pltpu.matmul_pop(sums[mxu])
+            for units in range(low, low + 2 * skew + 1):
+                pl.when(count_of(tm) == units)(functools.partial(reduce, units, *sums))
+            value = None
+            for mxu in range(2):
+                both = pltpu.matmul_pop(sums[mxu])
+                both = both[:pairs, :SHELLS] + both[pairs:, SHELLS:]
+                value = both if value is None else value + both
+            mine[...] = value
+
+        pl.run_scoped(multiply, *(pltpu.ACC(mxu)((2 * pairs, 2 * SHELLS), jnp.float32) for mxu in range(2)))
+
+        diagonal = mine[pl.ds(0, snaps, stride=snaps + 1), :]
         for t in range(snaps):
-            packs[t, :snaps] = row_of(pl.ds(t * snaps, snaps))
-            packs[t, snaps : 2 * snaps] = row_of(pl.ds(t, snaps, stride=snaps))
+            packs[t, :snaps] = mine[pl.ds(t * snaps, snaps), :]
+            packs[t, snaps : 2 * snaps] = mine[pl.ds(t, snaps, stride=snaps), :]
             packs[t, 2 * snaps :] = diagonal
         pl.semaphore_wait(far_ok, 1)
         for where in range(places):
@@ -351,7 +422,6 @@
     rows = blocks // snaps
     _, skew, low, slots = plan(rows)
     most = slots[-1][0] + 1
-    jobs = CORES * max(units for _, units, _ in slots)
     pairs = snaps * snaps
     high = 3 * snaps
     vel = velocity.reshape(3, 2, blocks, LANES).transpose(0, 2, 1, 3)
@@ -377,11 +447,11 @@
             pltpu.VMEM((CORES, most * PART, LANES), jnp.int32),
             pltpu.SMEM((snaps,), jnp.int32),
             pltpu.VMEM((CORES, snaps, 3, most * 2 * PART, LANES), jnp.bfloat16),
-            pltpu.VMEM((jobs, snaps * 3, 2 * PART, LANES), jnp.float32),
-            pltpu.VMEM((jobs, pairs * PART, LANES), jnp.float32),
-            pltpu.VMEM((jobs, pairs, PART * LANES), jnp.bfloat16),
-            pltpu.VMEM((CORES, SHELLS, most * PART * LANES), jnp.bfloat16),
-            pltpu.VMEM((2, pairs, SHELLS), jnp.float32),
+            pltpu.VMEM((2, snaps * 3, 2 * PART, LANES), jnp.float32),
+            pltpu.VMEM((2, pairs * PART, LANES), jnp.float32),
+            pltpu.VMEM((2, 2, 2 * pairs, 2 * LANES), jnp.bfloat16),
+            pltpu.VMEM((CORES, most, 2, 2 * SHELLS, 2 * LANES), jnp.bfloat16),
+            pltpu.VMEM((pairs, SHELLS), jnp.float32),
             pltpu.VMEM((snaps, high, SHELLS), jnp.float32),
             pltpu.VMEM((2 * snaps * places, high, SHELLS), jnp.float32),
             pltpu.VMEM((high, SHELLS), jnp.float32),
@@ -394,6 +464,7 @@
             pltpu.SemaphoreType.DMA((CORES * len(slots),)),
             pltpu.SemaphoreType.DMA,
             pltpu.SemaphoreType.DMA,
+            pltpu.SemaphoreType.REGULAR,
             pltpu.SemaphoreType.REGULAR,
             pltpu.SemaphoreType.REGULAR,
         ],

time: 14.7 us -> 14.3 us (0.973)
  Pallas kernels: 13.9 us -> 13.5 us
    pallas_call x1, Pallas kernels: 13.3 us -> 12.9 us  [body(): pl.pallas_call(functools.partial(kernel, snaps, slabs, rows), out_shape=(...]
where the time goes in v3:
time: 14.3 us; the launch traced here: 14.2 us
  Pallas kernels  13.5 us (94%)
  between operations  0.64 us (4%)
    pallas_call x1, Pallas kernels, body(): pl.pallas_call(functools.partial(kernel, snaps, slabs, rows), out_shape=(...  12.9 us
    pallas_call x1, Pallas kernels, body(): pl.pallas_call(put, out_shape=(jax.ShapeDtypeStruct((1, snaps, SHELLS), j...  0.6 us

profile of v3, /device:TPU:0, one launch (start us, length us, event | category | flops | bytes accessed | tf_op | source)
XLA Modules:
  0.0 14.2 jit_solution(13354332513146581518)
XLA Ops:
  0.6 12.9 %shard_map.50 = (f32[1,4,128]{2,1,0:T(4,128)S(1)}, f32[1,128]{1,0:T(1,128)S(1)}) custom-call(bf16[3,256,128]{2,1,0:T(8,128)(2,1)} %bitcast.6, s32[128,128]{1,0:T(8,128)} %bitcast.7, s32[4]{0:T(128)} %order_ref.1), custom_call_target="tpu_custom_call" | custom-call | tf_op jit(solution)/shard_map/pallas_call | solution.py:430
  13.6 0.6 %shard_map.51 = (f32[1,4,128]{2,1,0:T(4,128)}, f32[1,128]{1,0:T(1,128)}) custom-call(f32[1,4,128]{2,1,0:T(4,128)S(1)} %get-tuple-element.4.coh_ref, f32[1,128]{1,0:T(1,128)S(1)} %get-tuple-element.5.spec_ref), custom_call_target="tpu_custom_call" | custom-call | tf_op jit(solution)/shard_map/pallas_call | solution.py:475

commit v4 on v3

--- a/solution.py
+++ b/solution.py
@@ -20,8 +20,7 @@
     skew = 1 if base >= 3 else 0
     low = base - skew
     slots = [(0, low - 1, 0)] if low > 1 else []
-    slots += [(low - 1 + extra, 1, extra + 1) for extra in range(2 * skew)]
-    slots.append((low - 1 + 2 * skew, 1, 0))
+    slots += [(low - 1 + extra, 1, extra) for extra in range(2 * skew + 1)]
     return base, skew, low, slots
 
 
@@ -30,8 +29,8 @@
     vel_ref, ids_ref, order_ref,
     coh_ref, spec_ref,
     staged, ids, order, got, split, terms, lhs, hot, mine, packs, inbox, total, ready,
-    load_sem, stage_sem, ids_send, ids_recv, send_sem, recv_sem, pack_send, pack_recv,
-    near_ok, far_ok, late_ok,
+    load_sem, stage_sem, ids_recv, send_sem, recv_sem, pack_recv,
+    near_ok, far_ok,
 ):
     tm = lax.axis_index("tm")
     slab = lax.axis_index("slab")
@@ -41,6 +40,7 @@
     pairs = snaps * snaps
     blocks = rows * snaps
     base, skew, low, slots = plan(rows)
+    counts = range(low, low + 2 * skew + 1)
     hub = core == HUB
     leaf = core != HUB
     me = place * snaps + tm
@@ -71,10 +71,7 @@
         first = snap * base
         if skew:
             first = first + (jnp.where(snap == 0, 0, skew) if not isinstance(snap, int) else (skew if snap else 0))
-        at = slots[slot][0]
-        if slot == len(slots) - 1:
-            at = count_of(snap) - 1
-        return first + at
+        return first + slots[slot][0]
 
     def piece(start, units, scale):
         size = PART * scale
@@ -103,10 +100,18 @@
             else:
                 run(slot)
 
-    load_order = pltpu.make_async_copy(order_ref, order, load_sem.at[2])
-    for part in range(snaps):
-        span = pl.ds(part * 2 * rows, 2 * rows)
-        pltpu.make_async_copy(vel_ref.at[:, span], staged.at[:, span], stage_sem).start()
+    load_order = pltpu.make_async_copy(order_ref, order, load_sem.at[1])
+    lead = slots[0][1]
+    spans = [
+        [piece(source_of(snap, 0), lead, 2) for snap in range(snaps)],
+        [
+            piece(source_of(snap, 0) + lead, count_of(snap) - lead, 2)
+            for snap in range(snaps) if count_of(snap) > lead
+        ],
+    ]
+    for n, some in enumerate(spans):
+        for span in some:
+            pltpu.make_async_copy(vel_ref.at[:, span], staged.at[:, span], stage_sem).start()
 
     @pl.when(leaf)
     def _():
@@ -149,19 +154,30 @@
         at, units, _ = slots[slot]
         pltpu.make_async_copy(
             ids_ref.at[piece(source_of(tm, slot), units, 1)],
-            ids.at[HUB, pl.ds(at * PART, units * PART)], load_sem.at[1],
+            ids.at[HUB, pl.ds(at * PART, units * PART)], load_sem.at[0],
         ).start()
 
     for_slots(tm, load_ids)
 
     def drain_ids(ref, sem):
-        for units in range(low, low + 2 * skew + 1):
+        for units in counts:
             @pl.when(count_of(tm) == units)
             def _():
                 drain(ref.at[pl.ds(0, units * PART)], sem)
 
-    def exchange(peers):
-        for slot in range(len(slots)):
+    every = range(len(slots))
+
+    def bell(unit, slot):
+        rest = len(slots) + min(slot, 1)
+        if isinstance(unit, int):
+            return rest if unit == HUB else slot
+        return jnp.where(unit == HUB, rest, slot)
+
+
+    def exchange(peers, waits=False, chosen=every):
+        for slot in chosen:
+            if waits and slot == 0:
+                drain(staged, stage_sem)
             for peer in peers:
                 at, units, need = slots[slot]
 
@@ -169,7 +185,7 @@
                     send(
                         staged.at[:, piece(source_of(peer, slot), units, 2)],
                         got.at[core, tm, :, pl.ds(at * 2 * PART, units * 2 * PART)],
-                        send_sem, recv_sem.at[core * len(slots) + slot], hub_of(peer, place),
+                        send_sem, recv_sem.at[bell(core, slot)], hub_of(peer, place),
                     )
 
                 if need and isinstance(peer, int):
@@ -182,7 +198,7 @@
 
     @pl.when(leaf)
     def _():
-        drain_ids(ids.at[HUB], load_sem.at[1])
+        drain_ids(ids.at[HUB], load_sem.at[0])
 
         @pl.when(jnp.logical_or(gate, head))
         def _():
@@ -191,28 +207,26 @@
         @pl.when(jnp.logical_not(jnp.logical_or(gate, head)))
         def _():
             pl.semaphore_wait(barrier, snaps)
-
-        drain(staged, stage_sem)
 
         def ship_ids(slot):
             at, units, _ = slots[slot]
             span = pl.ds(at * PART, units * PART)
-            send(ids.at[HUB, span], ids.at[1 - HUB, span], ids_send, ids_recv, hub_of(tm, place))
+            send(ids.at[HUB, span], ids.at[1 - HUB, span], send_sem, ids_recv, hub_of(tm, place))
 
         for_slots(tm, ship_ids)
 
         @pl.when(head)
         def _():
-            exchange(list(range(1, last)) + [0])
+            exchange(list(range(1, last)) + [0], True)
             pl.semaphore_wait(barrier, 1)
             pl.semaphore_signal(
-                late_ok, inc=1, device_id=hub_of(tm, place), device_id_type=MESH
+                near_ok, inc=1, device_id=hub_of(tm, place), device_id_type=MESH
             )
             exchange([last])
 
         @pl.when(jnp.logical_not(head))
         def _():
-            exchange(others + [tm])
+            exchange(others + [tm], True)
 
         @pl.when(gate)
         def _():
@@ -240,15 +254,13 @@
                 near_ok, inc=1, device_id=leaf_of(tm, place), device_id_type=MESH
             )
 
-        drain(staged, stage_sem)
-
         @pl.when(head)
         def _():
-            exchange(list(range(1, last)))
+            exchange(list(range(1, last)), True, every[:1])
 
         @pl.when(jnp.logical_not(head))
         def _():
-            exchange(others)
+            exchange(others, True, every[:1])
 
         shell = lax.broadcasted_iota(jnp.int32, (SHELLS, LANES), 0)
 
@@ -266,21 +278,25 @@
                     same, 1.0, 0.0
                 ).astype(jnp.bfloat16)
 
-        drain_ids(ids.at[HUB], load_sem.at[1])
+        for units in counts:
+            @pl.when(count_of(tm) == units)
+            def _():
+                drain(hot.at[0, pl.ds(0, units), 0, pl.ds(0, 4 * PART)], load_sem.at[0])
+
         for_slots(tm, functools.partial(one_hot, HUB))
 
         @pl.when(head)
         def _():
-            pl.semaphore_wait(late_ok, 1)
+            exchange(list(range(1, last)), True, every[1:])
+            pl.semaphore_wait(near_ok, 1)
             exchange([last])
+
+        @pl.when(jnp.logical_not(head))
+        def _():
+            exchange(others, True, every[1:])
 
         drain_ids(ids.at[1 - HUB], ids_recv)
         for_slots(tm, functools.partial(one_hot, 1 - HUB))
-        for units in range(low, low + 2 * skew + 1):
-            @pl.when(count_of(tm) == units)
-            def _():
-                drain(got.at[HUB, 0, :, pl.ds(0, units * 2 * PART)], load_sem.at[0])
-
         def prepare(unit, at, row):
             span = pl.ds(at * 2 * PART, 2 * PART)
             real, imag = {}, {}
@@ -310,12 +326,14 @@
                 lhs[row, mxu, half * pairs : (half + 1) * pairs, lanes] = block.astype(jnp.bfloat16)
 
         def reduce(count, *sums):
+            live = [n for n, (_, _, need) in enumerate(slots) if low + need <= count]
+            groups = [(HUB, live[:1])] + [(1 - HUB, [n]) for n in live]
+            if live[1:]:
+                groups.insert(len(groups) - 1, (HUB, live[1:]))
             jobs = []
-            for slot, (at, units, need) in enumerate(slots):
-                if low + need <= count:
-                    for unit in (HUB, 1 - HUB):
-                        for step in range(units):
-                            jobs.append((unit, slot, at + step, step == 0))
+            for unit, some in groups:
+                spots = [slots[n][0] + step for n in some for step in range(slots[n][1])]
+                jobs += [(unit, some[0], at, len(spots) if at == spots[0] else 0) for at in spots]
 
             def stage(n):
                 unit, _, at, _ = jobs[n]
@@ -325,12 +343,9 @@
             stage(0)
             for n, (unit, slot, at, fresh) in enumerate(jobs):
                 if fresh:
-                    first, units, _ = slots[slot]
                     senders = snaps - 1 if unit == HUB else snaps
-                    span = pl.ds(first * 2 * PART, units * 2 * PART)
-                    drain(
-                        got.at[unit, pl.ds(0, senders), :, span], recv_sem.at[unit * len(slots) + slot]
-                    )
+                    span = pl.ds(at * 2 * PART, fresh * 2 * PART)
+                    drain(got.at[unit, pl.ds(0, senders), :, span], recv_sem.at[bell(unit, slot)])
                 if n + 1 < len(jobs):
                     stage(n + 1)
                 prepare(unit, at, n % 2)
@@ -340,7 +355,7 @@
         def multiply(*sums):
             for mxu in range(2):
                 pltpu.matmul_pop(sums[mxu])
-            for units in range(low, low + 2 * skew + 1):
+            for units in counts:
                 pl.when(count_of(tm) == units)(functools.partial(reduce, units, *sums))
             value = None
             for mxu in range(2):
@@ -359,11 +374,11 @@
         pl.semaphore_wait(far_ok, 1)
         for where in range(places):
             for snap in range(snaps):
-                send(packs.at[snap], inbox.at[me], pack_send, pack_recv, leaf_of(snap, where))
+                send(packs.at[snap], inbox.at[me], send_sem, pack_recv, leaf_of(snap, where))
 
                 @pl.when(me != where * snaps + snap)
                 def _():
-                    send(packs.at[snap], inbox.at[me], pack_send, pack_recv, hub_of(snap, where))
+                    send(packs.at[snap], inbox.at[me], send_sem, pack_recv, hub_of(snap, where))
         inbox[me] = packs[tm]
         drain(inbox.at[pl.ds(0, snaps * places - 1)], pack_recv)
 
@@ -391,15 +406,15 @@
     @pl.when(leaf)
     def _():
         drain(staged, send_sem)
-        drain_ids(ids.at[HUB], ids_send)
+        drain_ids(ids.at[HUB], send_sem)
 
     @pl.when(hub)
     def _():
-        for units in range(low, low + 2 * skew + 1):
+        for units in counts:
             @pl.when(count_of(tm) == units)
             def _():
                 drain(staged.at[:, pl.ds(0, 2 * (blocks - units * PART))], send_sem)
-        drain(inbox.at[pl.ds(0, 2 * snaps * places - 1)], pack_send)
+        drain(inbox.at[pl.ds(0, 2 * snaps * places - 1)], send_sem)
 
 
 def put(coh_ref, spec_ref, coh_out, spec_out, sems):
@@ -456,15 +471,12 @@
             pltpu.VMEM((2 * snaps * places, high, SHELLS), jnp.float32),
             pltpu.VMEM((high, SHELLS), jnp.float32),
             pltpu.VMEM((snaps, SHELLS), jnp.float32),
-            pltpu.SemaphoreType.DMA((3,)),
+            pltpu.SemaphoreType.DMA((2,)),
             pltpu.SemaphoreType.DMA,
             pltpu.SemaphoreType.DMA,
             pltpu.SemaphoreType.DMA,
+            pltpu.SemaphoreType.DMA((len(slots) + 2,)),
             pltpu.SemaphoreType.DMA,
-            pltpu.SemaphoreType.DMA((CORES * len(slots),)),
-            pltpu.SemaphoreType.DMA,
-            pltpu.SemaphoreType.DMA,
-            pltpu.SemaphoreType.REGULAR,
             pltpu.SemaphoreType.REGULAR,
             pltpu.SemaphoreType.REGULAR,
         ],

time: 14.3 us -> 14.3 us (level)
  no operation moved by 1% of the time
where the time goes in v4:
time: 14.3 us; the launch traced here: 14.1 us
  Pallas kernels  13.4 us (94%)
  between operations  0.64 us (4%)
    pallas_call x1, Pallas kernels, body(): pl.pallas_call(functools.partial(kernel, snaps, slabs, rows), out_shape=(...  12.8 us
    pallas_call x1, Pallas kernels, body(): pl.pallas_call(put, out_shape=(jax.ShapeDtypeStruct((1, snaps, SHELLS), j...  0.6 us

profile of v4, /device:TPU:0, one launch (start us, length us, event | category | flops | bytes accessed | tf_op | source)
XLA Modules:
  0.0 14.1 jit_solution(18259128184269458926)
XLA Ops:
  0.6 12.8 %shard_map.50 = (f32[1,4,128]{2,1,0:T(4,128)S(1)}, f32[1,128]{1,0:T(1,128)S(1)}) custom-call(bf16[3,256,128]{2,1,0:T(8,128)(2,1)} %bitcast.6, s32[128,128]{1,0:T(8,128)} %bitcast.7, s32[4]{0:T(128)} %order_ref.1), custom_call_target="tpu_custom_call" | custom-call | tf_op jit(solution)/shard_map/pallas_call | solution.py:445
  13.5 0.6 %shard_map.51 = (f32[1,4,128]{2,1,0:T(4,128)}, f32[1,128]{1,0:T(1,128)}) custom-call(f32[1,4,128]{2,1,0:T(4,128)S(1)} %get-tuple-element.4.coh_ref, f32[1,128]{1,0:T(1,128)S(1)} %get-tuple-element.5.spec_ref), custom_call_target="tpu_custom_call" | custom-call | tf_op jit(solution)/shard_map/pallas_call | solution.py:487

commit v5 on v4

--- a/solution.py
+++ b/solution.py
@@ -101,17 +101,9 @@
                 run(slot)
 
     load_order = pltpu.make_async_copy(order_ref, order, load_sem.at[1])
-    lead = slots[0][1]
-    spans = [
-        [piece(source_of(snap, 0), lead, 2) for snap in range(snaps)],
-        [
-            piece(source_of(snap, 0) + lead, count_of(snap) - lead, 2)
-            for snap in range(snaps) if count_of(snap) > lead
-        ],
-    ]
-    for n, some in enumerate(spans):
-        for span in some:
-            pltpu.make_async_copy(vel_ref.at[:, span], staged.at[:, span], stage_sem).start()
+    for part in range(snaps):
+        span = pl.ds(part * 2 * rows, 2 * rows)
+        pltpu.make_async_copy(vel_ref.at[:, span], staged.at[:, span], stage_sem).start()
 
     @pl.when(leaf)
     def _():
@@ -417,15 +409,10 @@
         drain(inbox.at[pl.ds(0, 2 * snaps * places - 1)], send_sem)
 
 
-def put(coh_ref, spec_ref, coh_out, spec_out, sems):
-    copies = [
-        pltpu.make_async_copy(coh_ref, coh_out, sems.at[0]),
-        pltpu.make_async_copy(spec_ref, spec_out, sems.at[1]),
-    ]
-    for copy in copies:
-        copy.start()
-    for copy in copies:
-        copy.wait()
+def put(coh_ref, spec_ref, coh_out, spec_out, both, sem):
+    pltpu.make_async_copy(coh_ref, coh_out, sem).start()
+    pltpu.make_async_copy(spec_ref, spec_out, sem).start()
+    pltpu.make_async_copy(both, both, sem).wait()
 
 
 def body(velocity, shell_index, ref_order):
@@ -492,7 +479,7 @@
         ),
         in_specs=[pl.BlockSpec(memory_space=pltpu.VMEM)] * 2,
         out_specs=(pl.BlockSpec(memory_space=pl.ANY),) * 2,
-        scratch_shapes=[pltpu.SemaphoreType.DMA((2,))],
+        scratch_shapes=[pltpu.VMEM((snaps + 1, SHELLS), jnp.float32), pltpu.SemaphoreType.DMA],
     )(coherence, spectrum)
 
 

time: 14.3 us -> 14.2 us (level)
  no operation moved by 1% of the time
where the time goes in v5:
time: 14.2 us; the launch traced here: 14.1 us
  Pallas kernels  13.4 us (94%)
  between operations  0.64 us (5%)
    pallas_call x1, Pallas kernels, body(): pl.pallas_call(functools.partial(kernel, snaps, slabs, rows), out_shape=(...  12.8 us
    pallas_call x1, Pallas kernels, body(): pl.pallas_call(put, out_shape=(jax.ShapeDtypeStruct((1, snaps, SHELLS), j...  0.59 us

profile of v5, /device:TPU:0, one launch (start us, length us, event | category | flops | bytes accessed | tf_op | source)
XLA Modules:
  0.0 14.1 jit_solution(17134769308319321627)
XLA Ops:
  0.6 12.8 %shard_map.50 = (f32[1,4,128]{2,1,0:T(4,128)S(1)}, f32[1,128]{1,0:T(1,128)S(1)}) custom-call(bf16[3,256,128]{2,1,0:T(8,128)(2,1)} %bitcast.6, s32[128,128]{1,0:T(8,128)} %bitcast.7, s32[4]{0:T(128)} %order_ref.1), custom_call_target="tpu_custom_call" | custom-call | tf_op jit(solution)/shard_map/pallas_call | solution.py:432
  13.5 0.6 %shard_map.51 = (f32[1,4,128]{2,1,0:T(4,128)}, f32[1,128]{1,0:T(1,128)}) custom-call(f32[1,4,128]{2,1,0:T(4,128)S(1)} %get-tuple-element.4.coh_ref, f32[1,128]{1,0:T(1,128)S(1)} %get-tuple-element.5.spec_ref), custom_call_target="tpu_custom_call" | custom-call | tf_op jit(solution)/shard_map/pallas_call | solution.py:474
